TPU v7x, 256 devices: a 2x2x32 block of a 4x8x32 slice. The times are simulated.
256 devices in a mesh: groups: 4 (over y, x), seq: 32 (over z), head: 2 (over core).
Axes of the slice: x: 2, y: 2, z: 32, core: 2. Of those that a mesh axis runs over, the one named last changes fastest.
The devices are a block of a 4x8x32 slice.
Arguments:
- q_latent: bfloat16 [128, 64, 512], P(('groups', 'seq'), 'head'), parts along dimension 0, may hold values from -7.5 to 7.5
- q_rope: bfloat16 [128, 4096], P(('groups', 'seq'), 'head'), parts along dimension 0, may hold values from -7.5 to 7.5
- cache_latent: bfloat16 [24576, 64, 512], P(('groups', 'seq', 'head')), parts along dimension 0, may hold values from -10 to 10
- cache_rope: bfloat16 [24576, 4096], P(('groups', 'seq', 'head')), parts along dimension 0, may hold values from -6 to 6
- page_table: int32 [128, 192], P('groups'), parts along dimension 0, may hold values from 0 to 6143, as said below
- lengths: int32 [128], P('groups'), parts along dimension 0, may hold values from 1 to 12288, 235929 in all
Outputs:
- attended: bfloat16 [128, 64, 512], P(('groups', 'seq'), 'head'), parts along dimension 0
There are 4 independent parts, one for each index of `groups`. A program takes and returns all parts, laid end to end along the dimension named above; each array names one. Nothing has to cross between parts.
Inputs may be any that keep to these rules, and one draw needn't show every extreme that they name: `page_table`: device d of a group (d = seq index * 2 + head index) holds pool pages d * 96 to (d + 1) * 96 - 1. Each pool page is named exactly once. A request's logical pages k * 3 to (k + 1) * 3 - 1 lie on one device, and every device holds exactly one such run of every request. `lengths`: the newest token is counted.
All inputs are finite; a program needn't handle non-finite values.
Results may differ from a plain program's by a relative error of at most 0.0055.
Values may be sent and summed in bfloat16 or wider, within the bound.
No kernel may reach another device: no remote copies, remote signals or barrier semaphores. Data moves between devices by JAX's collectives and lax.ppermute only.
A program may use at most 128 MiB of HBM per device.

v0:
```python
import math

import jax
import jax.numpy as jnp
from jax import lax
from jax.sharding import PartitionSpec as P

ROPE = 64
NOPE = 128


MASKED_SCORE = -1e30


def joined_along(pieces, dim):
    lengths = list(pieces.shape[1:])
    lengths[dim] *= pieces.shape[0]
    return jnp.moveaxis(pieces, 0, dim).reshape(lengths)


def gather_together(arrays, axis, dims):
    line = jnp.concatenate([a.reshape(-1) for a in arrays])
    lines, at, gathered = (lax.all_gather(line, axis), 0, [])
    for a, dim in zip(arrays, dims):
        pieces = lines[:, at : at + a.size].reshape(-1, *a.shape)
        gathered.append(joined_along(pieces, dim))
        at += a.size
    return tuple(gathered)


def split_up(array, dim, count):
    before, after = (array.shape[:dim], array.shape[dim + 1 :])
    return jnp.moveaxis(array.reshape(*before, count, -1, *after), dim, 0)


def joined_exchange(array, axis, axes, splits, concats):
    sizes = [lax.axis_size(a) for a in axes]
    pieces = split_up(array, splits[0], sizes[0])
    pieces = jnp.moveaxis(split_up(pieces, splits[1] + 1, sizes[1]), 0, 1)
    inside = pieces.shape[2:]
    pieces = pieces.reshape(-1, *inside)
    pieces = lax.all_to_all(pieces, axis, split_axis=0, concat_axis=0, tiled=True)
    pieces = joined_along(pieces.reshape(*sizes, *inside), concats[0] + 1)
    return joined_along(pieces, concats[1])


def local(q_latent, q_rope, cache_latent, cache_rope, page_table, lengths):
    seq_count = lax.axis_size("seq")
    head_count = lax.axis_size("head")
    my_seq = lax.axis_index("seq")
    my_core = lax.axis_index("head")
    my_device = my_seq * head_count + my_core
    pool_pages, page_len, latent_width = cache_latent.shape
    rope_width = cache_rope.shape[1] // page_len
    request_count, page_slots = page_table.shape
    device_count = seq_count * head_count
    run_len = page_slots // device_count
    run_owner = page_table[:, ::run_len] // pool_pages
    device_ids = jnp.arange(device_count, dtype=jnp.int32)
    run_index = jnp.sum(jnp.where(run_owner == my_device, device_ids[None, :], 0), axis=1)
    offsets = jnp.arange(run_len, dtype=jnp.int32)
    slot_cols = run_index[:, None] * run_len + offsets[None, :]
    local_slots = jnp.take_along_axis(page_table, slot_cols, axis=1) - my_device * pool_pages
    flat_slots = local_slots.reshape(-1)
    picked_lat = cache_latent[flat_slots].reshape(request_count, run_len, page_len, latent_width)
    picked_rot = cache_rope[flat_slots].reshape(request_count, run_len, page_len * rope_width)
    score_scale = 1.0 / math.sqrt(NOPE + ROPE)
    token_ids = jnp.arange(page_len, dtype=jnp.int32)
    heads_part = gather_together((q_latent, q_rope), "head", (1, 1))
    all_lat, all_rot = (
        lax.all_gather(heads_part[0], "seq", axis=0, tiled=True),
        lax.all_gather(heads_part[1], "seq", axis=0, tiled=True),
    )
    head_total = all_lat.shape[1]
    all_rot = all_rot.reshape(request_count, head_total, rope_width)
    positions = (
        (run_index[:, None, None] * run_len + offsets[None, :, None]) * page_len
        + token_ids[None, None, :]
    ).reshape(request_count, run_len * page_len)
    live_mask = positions < lengths[:, None]
    key_rows = picked_lat.reshape(request_count, run_len * page_len, latent_width)
    rotary = picked_rot.reshape(request_count, run_len * page_len, rope_width)
    scores = jnp.einsum("rhd,rtd->rht", all_lat, key_rows, preferred_element_type=jnp.float32)
    scores = (
        scores + jnp.einsum("rhd,rtd->rht", all_rot, rotary, preferred_element_type=jnp.float32)
    ) * score_scale
    scores = jnp.where(live_mask[:, None, :], scores, MASKED_SCORE)
    row_max = jnp.max(scores, axis=2)
    exp_terms = jnp.where(live_mask[:, None, :], jnp.exp(scores - row_max[:, :, None]), 0.0)
    row_total = jnp.sum(exp_terms, axis=2)
    summed = jnp.einsum(
        "rht,rtd->rhd", exp_terms.astype(jnp.bfloat16), key_rows, preferred_element_type=jnp.float32
    )
    got_sum, got_max, got_total = (
        joined_exchange(summed[None], ("seq", "head"), ("seq", "head"), (1, 2), (0, 0)),
        joined_exchange(row_max[None], ("seq", "head"), ("seq", "head"), (1, 2), (0, 0)),
        joined_exchange(row_total[None], ("seq", "head"), ("seq", "head"), (1, 2), (0, 0)),
    )
    best_max = jnp.max(got_max, axis=0)
    shrink = jnp.exp(got_max - best_max[None])
    merged_total = jnp.sum(got_total * shrink, axis=0)
    merged_sum = jnp.sum(got_sum * shrink[:, :, :, None], axis=0)
    return (merged_sum / merged_total[:, :, None]).astype(jnp.bfloat16)


def solution(mesh):
    return jax.shard_map(
        local,
        mesh=mesh,
        in_specs=(
            P(("groups", "seq"), "head", None),
            P(("groups", "seq"), "head"),
            P(("groups", "seq", "head"), None, None),
            P(("groups", "seq", "head"), None),
            P("groups", None),
            P("groups"),
        ),
        out_specs=P(("groups", "seq"), "head", None),
        check_vma=False,
    )
```

profile of v0, /device:TPU:38, one launch (start us, length us, event | category | flops | bytes accessed | tf_op | source)
XLA Modules:
  0.0 625.6 jit_solution(223792705310521540)
XLA Ops:
  6.6 0.9 copy.20
  7.4 0.7 reduce.8
  8.2 1.9 all-gather
  11.0 1.1 slice.9
  12.4 1.5 gather_fusion.2
  14.5 77.8 %all-gather.1 = bf16[32,1,4096]{2,1,0:T(2,128)(2,1)S(1)} all-gather(bf16[1,1,4096]{2,1,0:T(2,128)(2,1)S(1)} %reshape.306), channel_id=1, replica_groups=mesh['groups'=4,'seq'=32,'head'=2] {'seq'}, dimensions={0}, use_global_device_ids=true | all-gather | bytes 270336 | tf_op jit(solution)/shard_map/all_gather | solution.py:72
  92.3 1.5 reduce.9
  94.4 1.0 gather_fusion.1
  95.4 2.6 reshape_reshape.12
  98.0 8.9 %gather_fusion = bf16[96,64,512]{2,1,0:T(8,128)(2,1)} fusion(bf16[96,64,512]{2,1,0:T(8,128)(2,1)} %param.8, s32[1024]{0:T(1024)S(1)} %pad_clamp_fusion), kind=kCustom, calls=%fused_computation | custom fusion | bytes 12583296 | tf_op jit(solution)/shard_map/gather | solution.py:65
  107.0 49.0 %all-gather.4.cloned.1.call-done = bf16[32,64,512]{2,1,0:T(8,128)(2,1)} async-done(((bf16[1,64,512]{2,1,0:T(8,128)(2,1)}), bf16[32,64,512]{2,1,0:T(8,128)(2,1)}) %all-gather.4.cloned.1.call-update) | async-done | bytes 2097168 | tf_op jit(solution)/shard_map/all_gather | solution.py:71
  156.0 5.6 fusion.16
  161.6 1.2 fusion.15
  162.9 0.7 reshape_transpose_transpose_reshape_transpose_reshape_broadcast_in_dim.10
  163.6 15.0 %all-to-all-start.1 = ((f32[64,1,1,32]{3,2,1,0:T(1,128)}), f32[64,1,1,32]{3,2,1,0:T(1,128)S(1)}, u32[]{:S(2)}, u32[]{:S(2)}) async-start(f32[64,1,1,32]{3,2,1,0:T(1,128)} %bitcast.7), calls=%async_computation.1 | async-start | bytes 65536 | tf_op jit(solution)/shard_map/all_to_all | solution.py:42
  178.6 0.7 fusion
  180.0 20.5 %all-to-all-done.1 = f32[64,1,1,32]{3,2,1,0:T(1,128)S(1)} async-done(((f32[64,1,1,32]{3,2,1,0:T(1,128)}), f32[64,1,1,32]{3,2,1,0:T(1,128)S(1)}, u32[]{:S(2)}, u32[]{:S(2)}) %all-to-all-start.1) | async-done | bytes 8224 | tf_op jit(solution)/shard_map/all_to_all | solution.py:42
  200.5 6.6 %all-to-all-start.2 = ((f32[64,1,1,32]{3,2,1,0:T(1,128)}), f32[64,1,1,32]{3,2,1,0:T(1,128)S(1)}, u32[]{:S(2)}, u32[]{:S(2)}) async-start(f32[64,1,1,32]{3,2,1,0:T(1,128)} %bitcast.12), calls=%async_computation.2 | async-start | bytes 65536 | tf_op jit(solution)/shard_map/all_to_all | solution.py:42
  207.2 6.1 fusion.2
  213.3 15.8 %all-to-all-done.2 = f32[64,1,1,32]{3,2,1,0:T(1,128)S(1)} async-done(((f32[64,1,1,32]{3,2,1,0:T(1,128)}), f32[64,1,1,32]{3,2,1,0:T(1,128)S(1)}, u32[]{:S(2)}, u32[]{:S(2)}) %all-to-all-start.2) | async-done | bytes 8224 | tf_op jit(solution)/shard_map/all_to_all | solution.py:42
  229.1 7.5 %all-to-all-start = ((f32[64,1,1,32,512]{4,3,2,1,0:T(8,128)}), f32[64,1,1,32,512]{4,3,2,1,0:T(8,128)}, u32[]{:S(2)}, u32[]{:S(2)}) async-start(f32[64,1,1,32,512]{4,3,2,1,0:T(8,128)} %bitcast.42), calls=%async_computation | async-start | bytes 8388608 | tf_op jit(solution)/shard_map/all_to_all | solution.py:42
  236.8 378.7 %all-to-all-done = f32[64,1,1,32,512]{4,3,2,1,0:T(8,128)} async-done(((f32[64,1,1,32,512]{4,3,2,1,0:T(8,128)}), f32[64,1,1,32,512]{4,3,2,1,0:T(8,128)}, u32[]{:S(2)}, u32[]{:S(2)}) %all-to-all-start) | async-done | bytes 4194336 | tf_op jit(solution)/shard_map/all_to_all | solution.py:42
  615.5 2.5 multiply_reduce_fusion
  618.0 0.7 fusion.7
  (37 shorter events, 3.2 us)
Async XLA Ops:
  6.5 87.8 %copy-start = (bf16[96,4096]{1,0:T(8,128)(2,1)S(1)}, bf16[96,4096]{1,0:T(8,128)(2,1)}, u32[]{:S(2)}) copy-start(bf16[96,4096]{1,0:T(8,128)(2,1)} %param.9) | copy-start | bytes 2359300
  6.6 5.8 copy-start.1
  6.6 149.4 %all-gather.4.cloned.1.call-start = ((), (), s32[]{:S(2)}) async-start(), calls=%async_computation.3 | async-start | bytes 2162688 | tf_op jit(solution)/shard_map/all_gather | solution.py:71
  98.0 8.9 %copy-start.3 = (s32[32]{0:T(128)S(1)}, s32[32]{0:T(128)}, u32[]{:S(2)}) copy-start(s32[32]{0:T(128)} %param.11) | copy-start | bytes 388
  156.0 5.6 copy-start.2
  163.6 37.0 %all-to-all-start.1 = ((f32[64,1,1,32]{3,2,1,0:T(1,128)}), f32[64,1,1,32]{3,2,1,0:T(1,128)S(1)}, u32[]{:S(2)}, u32[]{:S(2)}) async-start(f32[64,1,1,32]{3,2,1,0:T(1,128)} %bitcast.7), calls=%async_computation.1 | async-start | bytes 65536 | tf_op jit(solution)/shard_map/all_to_all | solution.py:42
  200.5 28.6 %all-to-all-start.2 = ((f32[64,1,1,32]{3,2,1,0:T(1,128)}), f32[64,1,1,32]{3,2,1,0:T(1,128)S(1)}, u32[]{:S(2)}, u32[]{:S(2)}) async-start(f32[64,1,1,32]{3,2,1,0:T(1,128)} %bitcast.12), calls=%async_computation.2 | async-start | bytes 65536 | tf_op jit(solution)/shard_map/all_to_all | solution.py:42
  229.1 386.3 %all-to-all-start = ((f32[64,1,1,32,512]{4,3,2,1,0:T(8,128)}), f32[64,1,1,32,512]{4,3,2,1,0:T(8,128)}, u32[]{:S(2)}, u32[]{:S(2)}) async-start(f32[64,1,1,32,512]{4,3,2,1,0:T(8,128)} %bitcast.42), calls=%async_computation | async-start | bytes 8388608 | tf_op jit(solution)/shard_map/all_to_all | solution.py:42
Sparse Core Ops, SparseCore 0:
  11.0 144.9 all-gather.3
where the time goes:
time: 626 us
  waiting for transfers between devices  464 us (74%)
  blocking collectives  79.7 us (13%)
  starting transfers between devices  29.1 us (5%)
  local copies, waits for them, and re-layouts  19.2 us (3%)
  between operations  13.6 us (2%)
  matrix products  13 us (2%)
  other arithmetic  6.78 us (1%)
    all_to_all x3, waiting for transfers between devices, joined_exchange(): lax.all_to_all(pieces, axis, split_axis=0, concat_axis=0, tiled=True)  415 us
    all_gather x1, blocking collectives, local(): lax.all_gather(heads_part[1], 'seq', axis=0, tiled=True)  77.8 us
    all_gather x1, waiting for transfers between devices, local(): lax.all_gather(heads_part[0], 'seq', axis=0, tiled=True)  49 us
    all_to_all x3, starting transfers between devices, joined_exchange(): lax.all_to_all(pieces, axis, split_axis=0, concat_axis=0, tiled=True)  29.1 us
  transfers between devices with their start and end apart: 4, of which 4 were waited for; matrix products, arithmetic and copies ran while one was open for 4% of the time, Pallas kernels for 0%

commit v1 on v0

v1 whole, which is shorter than its diff:
```python
import math

import jax
import jax.numpy as jnp
from jax import lax
from jax.experimental import pallas as pl
from jax.experimental.pallas import tpu as pltpu
from jax.sharding import PartitionSpec as P

ROPE = 64
NOPE = 128
LANES = 128
STAT_ROWS = 16
MASKED_SCORE = -1e30


def shift_from(array, offset, axis):
    count = lax.axis_size(axis)
    return lax.ppermute(array, axis, [((i + offset) % count, i) for i in range(count)])


def gathered_by_offset(block, axis):
    count = lax.axis_size(axis)
    far, mid = 11, 4
    assert count == 32
    first = [(0, block)]
    for step in (far, -far):
        first.append((step, shift_from(block, step, axis)))
    three = jnp.concatenate([b for _, b in first], axis=0)
    base = [o for o, _ in first]
    pieces, offsets = [three], list(base)
    for step in (mid, -mid):
        pieces.append(shift_from(three, step, axis))
        offsets += [o + step for o in base]
    nine = jnp.concatenate(pieces, axis=0)
    place = {o: i for i, o in enumerate(offsets)}
    plus = shift_from(nine, 1, axis)
    minus = shift_from(nine, -1, axis)
    skip_plus = jnp.concatenate([nine[place[o] : place[o] + 1] for o in (0, 7, 11)], axis=0)
    skip_minus = jnp.concatenate([nine[place[o] : place[o] + 1] for o in (0, -7, -11)], axis=0)
    plus_two = shift_from(skip_plus, 2, axis)
    minus_two = shift_from(skip_minus, -2, axis)
    parts = [nine, plus, minus, plus_two, minus_two]
    listed = list(offsets) + [o + 1 for o in offsets] + [o - 1 for o in offsets]
    listed += [2, 9, 13, -2, -9, -13]
    return parts, listed


def attention_kernel(
    run_len, request_ref, own_ref, partner_ref, own_live_ref, partner_live_ref, q_ref, *refs
):
    latents, ropes, out_ref = refs[: 2 * run_len], refs[2 * run_len : 4 * run_len], refs[-1]
    step = pl.program_id(0)
    own_live, partner_live = own_live_ref[step], partner_live_ref[step]
    packed = q_ref.shape[1] - STAT_ROWS
    page_len, width = latents[0].shape[1:]
    slabs = width // LANES
    heads = packed // slabs
    half = run_len * page_len

    def store_stats(shift, total):
        lane = lax.broadcasted_iota(jnp.int32, (heads, LANES), 1)
        high = total.astype(jnp.bfloat16).astype(jnp.float32)
        stats = jnp.where(lane == 0, shift, jnp.where(lane == 1, high, total - high))
        turned = stats.T[:STAT_ROWS].astype(jnp.bfloat16)
        out_ref[0, packed:, :heads] = turned

    @pl.when(own_live + partner_live > 0)
    def _():
        block = q_ref[0]
        query = jnp.concatenate(
            [block[c * heads : (c + 1) * heads] for c in range(slabs)], axis=1
        )
        rope = block[packed:]
        lane = lax.broadcasted_iota(jnp.int32, rope.shape, 1)
        zero = jnp.zeros_like(rope)
        query_rope = jnp.concatenate(
            [jnp.where(lane < ROPE, rope, zero), jnp.where(lane >= ROPE, rope, zero)], axis=0
        )
        keys = jnp.concatenate([ref[0] for ref in latents], axis=0)
        rotary = jnp.concatenate([ref[0] for ref in ropes], axis=0)
        over_width = (((1,), (1,)), ((), ()))
        scores = lax.dot_general(query, keys, over_width, preferred_element_type=jnp.float32)
        scores = scores + lax.dot_general(
            query_rope, rotary, over_width, preferred_element_type=jnp.float32
        )
        scores = scores * (1.0 / math.sqrt(NOPE + ROPE))
        column = lax.broadcasted_iota(jnp.int32, scores.shape, 1)
        live = column < jnp.where(column < half, own_live, half + partner_live)
        scores = jnp.where(live, scores, MASKED_SCORE)
        shift = jnp.max(scores, axis=1, keepdims=True)
        shift = shift.astype(jnp.bfloat16).astype(jnp.float32)
        probs = jnp.where(live, jnp.exp(scores - shift), 0.0)
        total = jnp.sum(probs, axis=1, keepdims=True)
        summed = jnp.dot(probs.astype(jnp.bfloat16), keys, preferred_element_type=jnp.float32)
        summed = summed.astype(jnp.bfloat16)
        for c in range(slabs):
            out_ref[0, c * heads : (c + 1) * heads, :] = summed[:, c * LANES : (c + 1) * LANES]
        store_stats(shift, total)

    @pl.when(own_live + partner_live == 0)
    def _():
        out_ref[0, :packed, :] = jnp.zeros((packed, LANES), out_ref.dtype)
        store_stats(
            jnp.full((heads, 1), MASKED_SCORE, jnp.float32), jnp.zeros((heads, 1), jnp.float32)
        )


def attention(tables, queries, own_lat, partner_lat, own_rot, partner_rot, run_len):
    steps, rows, _ = queries.shape
    page_len, width = own_lat.shape[1:]

    def page_spec(array, which, j):
        def index(step, request, own, partner, own_live, partner_live):
            return ((own, partner)[which][step * run_len + j], 0, 0)

        return pl.BlockSpec((1,) + array.shape[1:], index)

    both_lat, both_rot = (own_lat, partner_lat), (own_rot, partner_rot)
    specs = [pl.BlockSpec((1, rows, LANES), lambda step, *_: (step, 0, 0))]
    operands = [queries]
    for both in (both_lat, both_rot):
        for which in range(2):
            for j in range(run_len):
                specs.append(page_spec(both[which], which, j))
                operands.append(both[which])
    tokens = 2 * run_len * page_len
    heads = (rows - STAT_ROWS) * LANES // width
    return pl.pallas_call(
        lambda *refs: attention_kernel(run_len, *refs),
        out_shape=jax.ShapeDtypeStruct((steps, rows, LANES), jnp.bfloat16),
        grid_spec=pltpu.PrefetchScalarGridSpec(
            num_scalar_prefetch=len(tables),
            grid=(steps,),
            in_specs=specs,
            out_specs=pl.BlockSpec(
                (1, rows, LANES), lambda step, request, *_: (request[step], 0, 0)
            ),
        ),
        cost_estimate=pl.CostEstimate(
            flops=steps * tokens * heads * (4 * width + 4 * ROPE),
            bytes_accessed=steps * tokens * (width + LANES) * 2,
            transcendentals=steps * tokens * heads,
        ),
        name="attention",
    )(*tables, *operands)


def local(q_latent, q_rope, cache_latent, cache_rope, page_table, lengths):
    seq_count = lax.axis_size("seq")
    head_count = lax.axis_size("head")
    my_seq = lax.axis_index("seq")
    my_core = lax.axis_index("head")
    pool_pages, page_len, latent_width = cache_latent.shape
    rope_width = cache_rope.shape[1] // page_len
    request_count, page_slots = page_table.shape
    device_count = seq_count * head_count
    run_len = page_slots // device_count
    heads = q_latent.shape[1]
    slabs = latent_width // LANES

    slab_rows = [q_latent[0, :, c * LANES : (c + 1) * LANES] for c in range(slabs)]
    rope_rows = q_rope.reshape(2, heads // 2, rope_width)
    rope_rows = jnp.concatenate([rope_rows[0], rope_rows[1]], axis=1)
    block = jnp.concatenate(slab_rows + [rope_rows], axis=0)[None]

    swap = [(i, head_count - 1 - i) for i in range(head_count)]
    partner_lat = lax.ppermute(cache_latent, "head", swap)
    own_rot = cache_rope.reshape(pool_pages, page_len, rope_width)
    own_rot = jnp.concatenate([own_rot, own_rot], axis=2)
    partner_rot = lax.ppermute(own_rot, "head", swap)

    parts, offsets = gathered_by_offset(block, "seq")
    seen, keep = set(), []
    for i, o in enumerate(offsets):
        if o % seq_count not in seen:
            seen.add(o % seq_count)
            keep.append(i)
    queries = jnp.concatenate(parts, axis=0)
    if len(keep) < len(offsets):
        dropped = [i for i in range(len(offsets)) if i not in keep]
        pieces, at = [], 0
        for d in dropped + [len(offsets)]:
            pieces.append(queries[at:d])
            at = d + 1
        queries = jnp.concatenate(pieces, axis=0)
    kept = jnp.array([offsets[i] % seq_count for i in keep], jnp.int32)
    request = (my_seq + kept) % seq_count

    run_owner = page_table[:, ::run_len] // pool_pages
    run_ids = jnp.arange(device_count, dtype=jnp.int32)
    slots = page_table.reshape(request_count, device_count, run_len)

    def runs_on(device):
        here = run_owner == device
        run_index = jnp.sum(jnp.where(here, run_ids[None, :], 0), axis=1)
        pages = jnp.sum(jnp.where(here[:, :, None], slots, 0), axis=1) - device * pool_pages
        live = jnp.clip(lengths - run_index * run_len * page_len, 0, run_len * page_len)
        return pages[request].reshape(-1), live[request]

    own_pages, own_live = runs_on(my_seq * head_count + my_core)
    partner_pages, partner_live = runs_on(my_seq * head_count + head_count - 1 - my_core)

    partial = attention(
        (request, own_pages, partner_pages, own_live, partner_live),
        queries, cache_latent, partner_lat, own_rot, partner_rot, run_len,
    )
    got = lax.all_to_all(partial, "seq", split_axis=0, concat_axis=0, tiled=True)

    packed = slabs * heads
    stats = got[:, packed:, :heads].astype(jnp.float32)
    got_max = stats[:, 0]
    got_total = stats[:, 1] + stats[:, 2]
    shrink = jnp.exp(got_max - jnp.max(got_max, axis=0)[None])
    merged_total = jnp.sum(got_total * shrink, axis=0)
    got_sum = got[:, :packed].reshape(seq_count, slabs, heads, LANES).astype(jnp.float32)
    merged_sum = jnp.sum(got_sum * shrink[:, None, :, None], axis=0)
    merged = merged_sum / merged_total[None, :, None]
    merged = jnp.concatenate([merged[c] for c in range(slabs)], axis=1)
    return merged.astype(jnp.bfloat16)[None]


def solution(mesh):
    return jax.shard_map(
        local,
        mesh=mesh,
        in_specs=(
            P(("groups", "seq"), "head", None),
            P(("groups", "seq"), "head"),
            P(("groups", "seq", "head"), None, None),
            P(("groups", "seq", "head"), None),
            P("groups", None),
            P("groups"),
        ),
        out_specs=P(("groups", "seq"), "head", None),
        check_vma=False,
    )
```

time: 626 us -> 258 us (0.41)
  waiting for transfers between devices: 464 us -> 8.38 us
  blocking collectives: 79.7 us -> 135 us
  Pallas kernels: 0 us -> 29.4 us
  starting transfers between devices: 29.1 us -> 51.6 us
  between operations: 13.6 us -> 0.21 us
  matrix products: 13 us -> 0 us
    all_to_all x3 -> x0, waiting for transfers between devices: 415 us -> none  [joined_exchange(): lax.all_to_all(pieces, axis, split_axis=0, concat_axis=0, tiled=True)]
    all_to_all x0 -> x1, blocking collectives: none -> 135 us  [local(): lax.all_to_all(partial, 'seq', split_axis=0, concat_axis=0, tiled=True)]
    all_gather x2 -> x0, blocking collectives: 79.7 us -> none  [the longest x1 77.8 us: local(): lax.all_gather(heads_part[1], 'seq', axis=0, tiled=True)]
    ppermute x0 -> x10, starting transfers between devices: none -> 51.6 us  [the longest x8 51.3 us: shift_from(): lax.ppermute(array, axis, [((i + offset) % count, i) for i in range(count)])]
    all_gather x1 -> x0, waiting for transfers between devices: 49 us -> none  [local(): lax.all_gather(heads_part[0], 'seq', axis=0, tiled=True)]
    pallas_call x0 -> x1, Pallas kernels: none -> 29.4 us  [attention(): pl.pallas_call(lambda *refs: attention_kernel(run_len, *refs), out_shape=...]
    all_to_all x3 -> x0, starting transfers between devices: 29.1 us -> none  [joined_exchange(): lax.all_to_all(pieces, axis, split_axis=0, concat_axis=0, tiled=True)]
    dot_general x3 -> x0, matrix products: 13 us -> none  [the longest x1 6.14 us: local(): jnp.einsum('rht,rtd->rhd', exp_terms.astype(jnp.bfloat16), key_rows, pref...]
  transfers between devices with their start and end apart: 4 -> 10, of which waited for: 4 -> 3; matrix products, arithmetic and copies ran while one was open for 4% -> 11% of each run, Pallas kernels for 0% -> 0%
where the time goes in v1:
time: 258 us; the launch traced here: 255 us
  blocking collectives  135 us (52%)
  starting transfers between devices  51.6 us (20%)
  Pallas kernels  29.4 us (11%)
  local copies, waits for them, and re-layouts  25 us (10%)
  waiting for transfers between devices  8.38 us (3%)
  other arithmetic  5.19 us (2%)
    all_to_all x1, blocking collectives, local(): lax.all_to_all(partial, 'seq', split_axis=0, concat_axis=0, tiled=True)  135 us
    ppermute x8, starting transfers between devices, shift_from(): lax.ppermute(array, axis, [((i + offset) % count, i) for i in range(count)])  51.3 us
    pallas_call x1, Pallas kernels, attention(): pl.pallas_call(lambda *refs: attention_kernel(run_len, *refs), out_shape=...  29.4 us
    unnamed x21, local copies, waits for them, and re-layouts  11 us
    ppermute x8, waiting for transfers between devices, shift_from(): lax.ppermute(array, axis, [((i + offset) % count, i) for i in range(count)])  8.37 us
  transfers between devices with their start and end apart: 10, of which 3 were waited for; matrix products, arithmetic and copies ran while one was open for 11% of the time, Pallas kernels for 0%

profile of v1, /device:TPU:38, one launch (start us, length us, event | category | flops | bytes accessed | tf_op | source)
XLA Modules:
  0.0 255.1 jit_solution(16600274416244813936)
XLA Ops:
  3.8 20.1 %collective-permute-start.1 = (bf16[1,144,128]{2,1,0:T(8,128)(2,1)S(1)}, bf16[1,144,128]{2,1,0:T(8,128)(2,1)S(1)}, u32[]{:S(2)}, u32[]{:S(2)}) collective-permute-start(bf16[1,144,128]{2,1,0:T(8,128)(2,1)S(1)} %bitcast.20), channel_id=1, source_target_pairs={{42,0},{44,2},{46,4},{48,6},{50,8},{52,10},{54,12},{56,14},{58,16}... | collective-permute-start | bytes 110600 | tf_op jit(solution)/shard_map/ppermute | solution.py:19
  23.9 7.9 %collective-permute-start = (bf16[1,144,128]{2,1,0:T(8,128)(2,1)S(1)}, bf16[1,144,128]{2,1,0:T(8,128)(2,1)S(1)}, u32[]{:S(2)}, u32[]{:S(2)}) collective-permute-start(bf16[1,144,128]{2,1,0:T(8,128)(2,1)S(1)} %bitcast.21), channel_id=1, source_target_pairs={{22,0},{24,2},{26,4},{28,6},{30,8},{32,10},{34,12},{36,14},{38,16}... | collective-permute-start | bytes 110600 | tf_op jit(solution)/shard_map/ppermute | solution.py:19
  31.8 1.6 copy.30
  33.4 2.4 copy.31
  35.8 0.9 pad_maximum_fusion.refs_12_.refs_13_.refs_14_
  38.7 2.2 collective-permute-done
  40.9 6.5 %collective-permute-start.3 = (bf16[3,144,128]{2,1,0:T(8,128)(2,1)S(1)}, bf16[3,144,128]{2,1,0:T(8,128)(2,1)S(1)}, u32[]{:S(2)}, u32[]{:S(2)}) collective-permute-start(bf16[3,144,128]{2,1,0:T(8,128)(2,1)S(1)} %pad_maximum_fusion.6), channel_id=1, source_target_pairs={{56,0},{58,2},{60,4},{62,6},{0,8},{2,10},{4,12},{6,14},{8,16},{10,... | collective-permute-start | bytes 331784 | tf_op jit(solution)/shard_map/ppermute | solution.py:19
  47.4 1.7 collective-permute-start.2
  50.5 6.0 %collective-permute-done.2 = bf16[3,144,128]{2,1,0:T(8,128)(2,1)} collective-permute-done((bf16[3,144,128]{2,1,0:T(8,128)(2,1)S(1)}, bf16[3,144,128]{2,1,0:T(8,128)(2,1)}, u32[]{:S(2)}, u32[]{:S(2)}) %collective-permute-start.2) | collective-permute-done | bytes 110624 | tf_op jit(solution)/shard_map/ppermute | solution.py:19
  56.5 1.6 constant_dynamic-update-slice_fusion.6
  58.8 5.0 %collective-permute-start.4 = (bf16[9,144,128]{2,1,0:T(8,128)(2,1)}, bf16[9,144,128]{2,1,0:T(8,128)(2,1)}, u32[]{:S(2)}, u32[]{:S(2)}) collective-permute-start(bf16[9,144,128]{2,1,0:T(8,128)(2,1)} %get-tuple-element.19), channel_id=1, source_target_pairs={{2,0},{4,2},{6,4},{8,6},{10,8},{12,10},{14,12},{16,14},{18,16},{20... | collective-permute-start | bytes 995336 | tf_op jit(solution)/shard_map/ppermute | solution.py:19
  64.3 6.9 %collective-permute-start.5 = (bf16[9,144,128]{2,1,0:T(8,128)(2,1)}, bf16[9,144,128]{2,1,0:T(8,128)(2,1)}, u32[]{:S(2)}, u32[]{:S(2)}) collective-permute-start(bf16[9,144,128]{2,1,0:T(8,128)(2,1)} %get-tuple-element.19), channel_id=1, source_target_pairs={{62,0},{0,2},{2,4},{4,6},{6,8},{8,10},{10,12},{12,14},{14,16},{16,... | collective-permute-start | bytes 995336 | tf_op jit(solution)/shard_map/ppermute | solution.py:19
  71.2 1.2 gather_fusion.3
  72.4 1.2 gather_fusion.2
  76.2 1.4 slice.95
  77.6 0.8 fusion
  78.6 2.9 %collective-permute-start.7 = (bf16[3,144,128]{2,1,0:T(8,128)(2,1)S(1)}, bf16[3,144,128]{2,1,0:T(8,128)(2,1)S(1)}, u32[]{:S(2)}, u32[]{:S(2)}) collective-permute-start(bf16[3,144,128]{2,1,0:T(8,128)(2,1)S(1)} %get-tuple-element.30), channel_id=1, source_target_pairs={{60,0},{62,2},{0,4},{2,6},{4,8},{6,10},{8,12},{10,14},{12,16},{14,... | collective-permute-start | bytes 331784 | tf_op jit(solution)/shard_map/ppermute | solution.py:19
  81.5 1.8 constant_dynamic-update-slice_fusion.11
  83.2 1.7 constant_dynamic-update-slice_fusion.10
  85.0 1.3 slice.93
  86.4 1.1 pad_maximum_fusion.1.refs_5_
  87.5 1.2 copy-done.1
  88.8 29.4 %attention.1 = bf16[32,144,128]{2,1,0:T(8,128)(2,1)} custom-call(s32[32]{0:T(128)} %get-tuple-element.16.refs_0_, s32[96]{0:T(128)} %reshape.89.refs_1_, s32[96]{0:T(128)} %reshape.90.refs_2_, s32[32]{0:T(128)} %gather_fusion.2, s32[32]{0:T(128)} %gather_fusion.3, bf16[32,144,128]{2,1,0:T(8,128)(2,1)} %pad_maximum_fusion.1.refs_5_, ...), custom_call_target="tpu_custom_call" | custom-call | flops 905969664 | bytes 15728640 | tf_op jit(solution)/shard_map/attention/pallas_call | solution.py:129
  118.2 135.3 %all_to_all.5 = bf16[32,144,128]{2,1,0:T(8,128)(2,1)S(1)} all-to-all(bf16[32,144,128]{2,1,0:T(8,128)(2,1)} %attention.1), channel_id=1, replica_groups=mesh['groups'=4,'seq'=32,'head'=2] {'seq'}, dimensions={0} | all-to-all | bytes 2359296 | tf_op jit(solution)/shard_map/all_to_all | solution.py:208
  (61 shorter events, 12.7 us)
Async XLA Ops:
  0.0 87.5 %collective-permute-start.8 = (bf16[96,64,512]{2,1,0:T(8,128)(2,1)}, bf16[96,64,512]{2,1,0:T(8,128)(2,1)}, u32[]{:S(2)}, u32[]{:S(2)}) collective-permute-start(bf16[96,64,512]{2,1,0:T(8,128)(2,1)} %refs_8_.1), channel_id=1, source_target_pairs={{0,1},{1,0},{2,3},{3,2},{4,5},{5,4},{6,7},{7,6},{8,9},{9,8},{10,11... | collective-permute-start | bytes 18874376 | tf_op jit(solution)/shard_map/ppermute | solution.py:168
  3.8 34.9 %collective-permute-start.1 = (bf16[1,144,128]{2,1,0:T(8,128)(2,1)S(1)}, bf16[1,144,128]{2,1,0:T(8,128)(2,1)S(1)}, u32[]{:S(2)}, u32[]{:S(2)}) collective-permute-start(bf16[1,144,128]{2,1,0:T(8,128)(2,1)S(1)} %bitcast.20), channel_id=1, source_target_pairs={{42,0},{44,2},{46,4},{48,6},{50,8},{52,10},{54,12},{56,14},{58,16}... | collective-permute-start | bytes 110600 | tf_op jit(solution)/shard_map/ppermute | solution.py:19
  23.9 16.9 %collective-permute-start = (bf16[1,144,128]{2,1,0:T(8,128)(2,1)S(1)}, bf16[1,144,128]{2,1,0:T(8,128)(2,1)S(1)}, u32[]{:S(2)}, u32[]{:S(2)}) collective-permute-start(bf16[1,144,128]{2,1,0:T(8,128)(2,1)S(1)} %bitcast.21), channel_id=1, source_target_pairs={{22,0},{24,2},{26,4},{28,6},{30,8},{32,10},{34,12},{36,14},{38,16}... | collective-permute-start | bytes 110600 | tf_op jit(solution)/shard_map/ppermute | solution.py:19
  35.8 1.3 copy-start.2
  35.8 2.9 %copy-start.3 = (s32[32]{0:T(128)S(1)}, s32[32]{0:T(128)}, u32[]{:S(2)}) copy-start(s32[32]{0:T(128)} %param.12) | copy-start | bytes 388
  36.7 38.9 %copy-start = (bf16[96,64,128]{2,1,0:T(8,128)(2,1)}, bf16[96,64,128]{2,1,0:T(8,128)(2,1)S(1)}, u32[]{:S(2)}) copy-start(bf16[96,64,128]{2,1,0:T(8,128)(2,1)S(1)} %pad_maximum_fusion.refs_12_.refs_13_.refs_14_) | copy-start | bytes 4718596
  36.7 27.1 %copy-start.4 = (s32[32]{0:T(128)S(1)}, s32[32]{0:T(128)}, u32[]{:S(2)}) copy-start(s32[32]{0:T(128)} %constant.53.clone) | copy-start | bytes 388
  36.7 50.8 %collective-permute-start.9 = (bf16[96,64,128]{2,1,0:T(8,128)(2,1)S(1)}, bf16[96,64,128]{2,1,0:T(8,128)(2,1)S(1)}, u32[]{:S(2)}, u32[]{:S(2)}) collective-permute-start(bf16[96,64,128]{2,1,0:T(8,128)(2,1)S(1)} %pad_maximum_fusion.refs_12_.refs_13_.refs_14_), channel_id=1, source_target_pairs={{0,1},{1,0},{2,3},{3,2},{4,5},{5,4},{6,7},{7,6},{8,9},{9,8},{10,11... | collective-permute-start | bytes 4718600 | tf_op jit(solution)/shard_map/ppermute | solution.py:171
  40.9 17.2 %collective-permute-start.3 = (bf16[3,144,128]{2,1,0:T(8,128)(2,1)S(1)}, bf16[3,144,128]{2,1,0:T(8,128)(2,1)S(1)}, u32[]{:S(2)}, u32[]{:S(2)}) collective-permute-start(bf16[3,144,128]{2,1,0:T(8,128)(2,1)S(1)} %pad_maximum_fusion.6), channel_id=1, source_target_pairs={{56,0},{58,2},{60,4},{62,6},{0,8},{2,10},{4,12},{6,14},{8,16},{10,... | collective-permute-start | bytes 331784 | tf_op jit(solution)/shard_map/ppermute | solution.py:19
  47.4 9.1 %collective-permute-start.2 = (bf16[3,144,128]{2,1,0:T(8,128)(2,1)S(1)}, bf16[3,144,128]{2,1,0:T(8,128)(2,1)}, u32[]{:S(2)}, u32[]{:S(2)}) collective-permute-start(bf16[3,144,128]{2,1,0:T(8,128)(2,1)S(1)} %pad_maximum_fusion.6), channel_id=1, source_target_pairs={{8,0},{10,2},{12,4},{14,6},{16,8},{18,10},{20,12},{22,14},{24,16},... | collective-permute-start | bytes 331784 | tf_op jit(solution)/shard_map/ppermute | solution.py:19
  58.8 19.7 %collective-permute-start.4 = (bf16[9,144,128]{2,1,0:T(8,128)(2,1)}, bf16[9,144,128]{2,1,0:T(8,128)(2,1)}, u32[]{:S(2)}, u32[]{:S(2)}) collective-permute-start(bf16[9,144,128]{2,1,0:T(8,128)(2,1)} %get-tuple-element.19), channel_id=1, source_target_pairs={{2,0},{4,2},{6,4},{8,6},{10,8},{12,10},{14,12},{16,14},{18,16},{20... | collective-permute-start | bytes 995336 | tf_op jit(solution)/shard_map/ppermute | solution.py:19
  64.3 18.9 %collective-permute-start.5 = (bf16[9,144,128]{2,1,0:T(8,128)(2,1)}, bf16[9,144,128]{2,1,0:T(8,128)(2,1)}, u32[]{:S(2)}, u32[]{:S(2)}) collective-permute-start(bf16[9,144,128]{2,1,0:T(8,128)(2,1)} %get-tuple-element.19), channel_id=1, source_target_pairs={{62,0},{0,2},{2,4},{4,6},{6,8},{8,10},{10,12},{12,14},{14,16},{16,... | collective-permute-start | bytes 995336 | tf_op jit(solution)/shard_map/ppermute | solution.py:19
  78.4 7.8 %collective-permute-start.6 = (bf16[3,144,128]{2,1,0:T(8,128)(2,1)S(1)}, bf16[3,144,128]{2,1,0:T(8,128)(2,1)S(1)}, u32[]{:S(2)}, u32[]{:S(2)}) collective-permute-start(bf16[3,144,128]{2,1,0:T(8,128)(2,1)S(1)} %get-tuple-element.29), channel_id=1, source_target_pairs={{4,0},{6,2},{8,4},{10,6},{12,8},{14,10},{16,12},{18,14},{20,16},{2... | collective-permute-start | bytes 331784 | tf_op jit(solution)/shard_map/ppermute | solution.py:19
  78.6 7.8 %collective-permute-start.7 = (bf16[3,144,128]{2,1,0:T(8,128)(2,1)S(1)}, bf16[3,144,128]{2,1,0:T(8,128)(2,1)S(1)}, u32[]{:S(2)}, u32[]{:S(2)}) collective-permute-start(bf16[3,144,128]{2,1,0:T(8,128)(2,1)S(1)} %get-tuple-element.30), channel_id=1, source_target_pairs={{60,0},{62,2},{0,4},{2,6},{4,8},{6,10},{8,12},{10,14},{12,16},{14,... | collective-permute-start | bytes 331784 | tf_op jit(solution)/shard_map/ppermute | solution.py:19
  87.5 1.2 copy-start.1

commit v2 on v0

v2 whole, which is shorter than its diff:
```python
import math

import jax
import jax.numpy as jnp
from jax import lax
from jax.experimental import pallas as pl
from jax.experimental.pallas import tpu as pltpu
from jax.sharding import PartitionSpec as P

ROPE = 64
NOPE = 128
LANES = 128
STAT_ROWS = 16
MASKED_SCORE = -1e30

FAR = (0, 6, 13, -13, -6)
NEAR = {
    1: FAR,
    -1: FAR,
    2: FAR,
    -2: FAR,
    3: (0, 6, 13, -13),
    -3: (0, 13, -6),
}

VMEM = pl.BlockSpec(memory_space=pltpu.VMEM)
HBM = pl.BlockSpec(memory_space=pltpu.HBM)
LIMIT = pltpu.CompilerParams(vmem_limit_bytes=12 << 20)
ATTENTION_LIMIT = pltpu.CompilerParams(vmem_limit_bytes=50 << 20)


def shift_from(array, offset, axis):
    count = lax.axis_size(axis)
    return lax.ppermute(array, axis, [((i + offset) % count, i) for i in range(count)])


def parts_of(x, count):
    parts = []
    for _ in range(count - 1):
        high = x.astype(jnp.bfloat16).astype(jnp.float32)
        parts.append(high)
        x = x - high
    return parts + [x]


def pack_kernel(q_ref, rope_ref, out_ref):
    heads, width = q_ref.shape[1:]
    for c in range(width // LANES):
        out_ref[0, c * heads : (c + 1) * heads, :] = q_ref[0, :, c * LANES : (c + 1) * LANES]
    out_ref[0, heads * width // LANES :, :] = rope_ref[...]


def attention_kernel(offsets, run_len, count, table_ref, q_ref, *refs):
    caches, (out_ref, lat_buf, rot_buf, sems) = refs[:4], refs[4:]
    own_lat, partner_lat, own_rot, partner_rot = caches
    page_len, width = own_lat.shape[1:]
    packed = q_ref.shape[1] - STAT_ROWS
    slabs = width // LANES
    heads = packed // slabs
    half = run_len * page_len
    entry = 2 * (run_len + 1)
    me = table_ref[count * entry]

    def copies(g):
        request = lax.rem(me + offsets[g] % count, count)
        made = []
        for which in range(2):
            for j in range(run_len):
                page = table_ref[request * entry + which * (run_len + 1) + j]
                slot = which * run_len + j
                rows = pl.ds(slot * page_len, page_len)
                for kind, (source, buf) in enumerate(
                    (((own_lat, partner_lat)[which], lat_buf), ((own_rot, partner_rot)[which], rot_buf))
                ):
                    made.append(
                        pltpu.make_async_copy(
                            source.at[page], buf.at[g, rows], sems.at[g, 2 * slot + kind]
                        )
                    )
        return request, made

    started = []
    for g in range(len(offsets)):
        request, made = copies(g)
        for copy in made:
            copy.start()
        started.append((request, made))

    lane = lax.broadcasted_iota(jnp.int32, (heads, LANES), 1)
    rope_lane = lax.broadcasted_iota(jnp.int32, (STAT_ROWS, LANES), 1)
    column = lax.broadcasted_iota(jnp.int32, (heads, 2 * half), 1)
    over_width = (((1,), (1,)), ((), ()))
    for g in range(len(offsets)):
        request, made = started[g]
        own_live = table_ref[request * entry + run_len]
        partner_live = table_ref[request * entry + 2 * run_len + 1]
        query = jnp.concatenate(
            [q_ref[g, c * heads : (c + 1) * heads, :] for c in range(slabs)], axis=1
        )
        rope = q_ref[g, packed:, :]
        zero = jnp.zeros_like(rope)
        query_rope = jnp.concatenate(
            [jnp.where(rope_lane < ROPE, rope, zero), jnp.where(rope_lane >= ROPE, rope, zero)],
            axis=0,
        )
        for copy in made:
            copy.wait()
        keys, rotary = lat_buf[g], rot_buf[g]
        scores = lax.dot_general(query, keys, over_width, preferred_element_type=jnp.float32)
        scores = scores + lax.dot_general(
            query_rope, rotary, over_width, preferred_element_type=jnp.float32
        )
        scores = scores * (1.0 / math.sqrt(NOPE + ROPE))
        live = column < jnp.where(column < half, own_live, half + partner_live)
        scores = jnp.where(live, scores, MASKED_SCORE)
        top = jnp.max(scores, axis=1, keepdims=True)
        probs = jnp.where(live, jnp.exp(scores - top), 0.0)
        total = jnp.sum(probs, axis=1, keepdims=True)
        summed = jnp.dot(probs.astype(jnp.bfloat16), keys, preferred_element_type=jnp.float32)
        summed = summed.astype(jnp.bfloat16)
        for c in range(slabs):
            out_ref[g, c * heads : (c + 1) * heads, :] = summed[:, c * LANES : (c + 1) * LANES]
        stats = jnp.zeros((heads, LANES), jnp.float32)
        for i, part in enumerate(parts_of(top, 3) + parts_of(total, 2)):
            stats = jnp.where(lane == i, part, stats)
        out_ref[g, packed:, :] = jnp.zeros((STAT_ROWS, LANES), out_ref.dtype)
        out_ref[g, packed:, :heads] = stats.T[:STAT_ROWS].astype(out_ref.dtype)


def attention(offsets, table, queries, caches, run_len, count):
    groups, rows, _ = queries.shape
    page_len, width = caches[0].shape[1:]
    tokens = 2 * run_len * page_len
    heads = (rows - STAT_ROWS) * LANES // width
    work = groups * tokens
    return pl.pallas_call(
        lambda *refs: attention_kernel(offsets, run_len, count, *refs),
        out_shape=jax.ShapeDtypeStruct((groups, rows, LANES), jnp.bfloat16),
        in_specs=[pl.BlockSpec(memory_space=pltpu.SMEM), VMEM] + [HBM] * 4,
        out_specs=VMEM,
        scratch_shapes=[
            pltpu.VMEM((groups, tokens, width), jnp.bfloat16),
            pltpu.VMEM((groups, tokens, LANES), jnp.bfloat16),
            pltpu.SemaphoreType.DMA((groups, 4 * run_len)),
        ],
        cost_estimate=pl.CostEstimate(
            flops=work * heads * (4 * width + 4 * ROPE),
            bytes_accessed=work * (width + LANES) * 2,
            transcendentals=work * heads,
        ),
        compiler_params=ATTENTION_LIMIT,
        name="attention",
    )(table, queries, *caches)


def merge_blocks(blocks, packed, heads, final):
    rows = [ref[i, packed:, :].astype(jnp.float32) for ref, i in blocks]
    tops = [r[0:1] + r[1:2] + r[2:3] for r in rows]
    totals = [r[3:4] + r[4:5] for r in rows]
    best = tops[0]
    for top in tops[1:]:
        best = jnp.maximum(best, top)
    weights = [jnp.exp(top - best) for top in tops]
    total = sum(w * t for w, t in zip(weights, totals))
    if final:
        weights = [w / total for w in weights]
    padded = weights + [jnp.zeros_like(best)] * (8 - len(weights))
    columns = jnp.concatenate(padded, axis=0).T
    columns = [columns[:heads, k : k + 1] for k in range(len(blocks))]
    slabs = []
    for c in range(packed // heads):
        slab = 0.0
        for column, (ref, i) in zip(columns, blocks):
            slab += column * ref[i, c * heads : (c + 1) * heads, :].astype(jnp.float32)
        slabs.append(slab.astype(jnp.bfloat16))
    if final:
        return slabs, None
    stats = parts_of(best, 3) + parts_of(total, 2)
    stats += [jnp.zeros((STAT_ROWS - len(stats), LANES), jnp.float32)]
    return slabs, jnp.concatenate(stats, axis=0).astype(jnp.bfloat16)


def near_merge_kernel(heads, sources, *refs):
    inputs, outs = refs[: len(sources)], refs[len(sources) :]
    packed = outs[0].shape[1] - STAT_ROWS
    for o, out_ref in zip(FAR, outs):
        blocks = [(ref, held.index(o)) for ref, held in zip(inputs, sources) if o in held]
        slabs, stats = merge_blocks(blocks, packed, heads, False)
        for c, slab in enumerate(slabs):
            out_ref[0, c * heads : (c + 1) * heads, :] = slab
        out_ref[0, packed:, :] = stats


def far_merge_kernel(*refs):
    inputs, out_ref = refs[:-1], refs[-1]
    heads = out_ref.shape[1]
    packed = inputs[0].shape[1] - STAT_ROWS
    slabs, _ = merge_blocks([(ref, 0) for ref in inputs], packed, heads, True)
    for c, slab in enumerate(slabs):
        out_ref[0, :, c * LANES : (c + 1) * LANES] = slab


def local(q_latent, q_rope, cache_latent, cache_rope, page_table, lengths):
    seq_count = lax.axis_size("seq")
    head_count = lax.axis_size("head")
    my_seq = lax.axis_index("seq")
    my_core = lax.axis_index("head")
    pool_pages, page_len, latent_width = cache_latent.shape
    rope_width = cache_rope.shape[1] // page_len
    request_count, page_slots = page_table.shape
    device_count = seq_count * head_count
    run_len = page_slots // device_count
    heads = q_latent.shape[1]
    reached = {o % seq_count for o in FAR} | {(o + d) % seq_count for d in NEAR for o in NEAR[d]}
    assert len(reached) == seq_count == len(FAR) + sum(len(held) for held in NEAR.values())

    rope_rows = q_rope.reshape(2, heads // 2, rope_width)
    rope_rows = jnp.concatenate([rope_rows[0], rope_rows[1]], axis=1)
    block_shape = (1, heads * latent_width // LANES + STAT_ROWS, LANES)
    block = pl.pallas_call(
        pack_kernel,
        out_shape=jax.ShapeDtypeStruct(block_shape, jnp.bfloat16),
        in_specs=[VMEM] * 2,
        out_specs=VMEM,
        compiler_params=LIMIT,
        name="pack",
    )(q_latent, rope_rows)

    swap = [(i, head_count - 1 - i) for i in range(head_count)]
    partner_lat = lax.ppermute(cache_latent, "head", swap)
    own_rot = cache_rope.reshape(pool_pages, page_len, rope_width)
    own_rot = jnp.concatenate([own_rot, own_rot], axis=2)
    partner_rot = lax.ppermute(own_rot, "head", swap)
    caches = (cache_latent, partner_lat, own_rot, partner_rot)

    run_owner = page_table[:, ::run_len] // pool_pages
    run_ids = jnp.arange(device_count, dtype=jnp.int32)
    slots = page_table.reshape(request_count, device_count, run_len)

    def runs_on(device):
        here = run_owner == device
        run_index = jnp.sum(jnp.where(here, run_ids[None, :], 0), axis=1)
        pages = jnp.sum(jnp.where(here[:, :, None], slots, 0), axis=1) - device * pool_pages
        live = jnp.clip(lengths - run_index * run_len * page_len, 0, run_len * page_len)
        return [pages, live[:, None]]

    entries = runs_on(my_seq * head_count + my_core)
    entries += runs_on(my_seq * head_count + head_count - 1 - my_core)
    table = jnp.concatenate(entries, axis=1).astype(jnp.int32).reshape(-1)
    table = jnp.concatenate([table, my_seq.astype(jnp.int32)[None]])

    def attend(offsets, queries):
        return attention(offsets, table, queries, caches, run_len, seq_count)

    far_blocks = [block if o == 0 else shift_from(block, o, "seq") for o in FAR]
    far = jnp.concatenate(far_blocks, axis=0)

    def chosen(held):
        return far if held == FAR else jnp.concatenate([far_blocks[FAR.index(o)] for o in held])

    near = {d: shift_from(chosen(held), d, "seq") for d, held in NEAR.items()}
    partials, sources = [attend(FAR, far)], [FAR]
    for d, held in NEAR.items():
        partial = attend(tuple(o + d for o in held), near[d])
        partials.append(shift_from(partial, -d, "seq"))
        sources.append(held)

    merged = pl.pallas_call(
        lambda *refs: near_merge_kernel(heads, sources, *refs),
        out_shape=[jax.ShapeDtypeStruct(block_shape, jnp.bfloat16)] * len(FAR),
        in_specs=[VMEM] * len(sources),
        out_specs=[VMEM] * len(FAR),
        compiler_params=LIMIT,
        name="near_merge",
    )(*partials)
    arrived = [b if o == 0 else shift_from(b, -o, "seq") for o, b in zip(FAR, merged)]
    return pl.pallas_call(
        far_merge_kernel,
        out_shape=jax.ShapeDtypeStruct((1, heads, latent_width), jnp.bfloat16),
        in_specs=[VMEM] * len(arrived),
        out_specs=VMEM,
        compiler_params=LIMIT,
        name="far_merge",
    )(*arrived)


def solution(mesh):
    return jax.shard_map(
        local,
        mesh=mesh,
        in_specs=(
            P(("groups", "seq"), "head", None),
            P(("groups", "seq"), "head"),
            P(("groups", "seq", "head"), None, None),
            P(("groups", "seq", "head"), None),
            P("groups", None),
            P("groups"),
        ),
        out_specs=P(("groups", "seq"), "head", None),
        check_vma=False,
    )
```

time: 626 us -> 172 us (0.27)
  the two profiles are of different devices: /device:TPU:38 before, /device:TPU:100 now
where the time goes in v2:
time: 172 us
  starting transfers between devices  88.8 us (52%)
  waiting for transfers between devices  35.4 us (21%)
  Pallas kernels  35 us (20%)
  local copies, waits for them, and re-layouts  8 us (5%)
  other arithmetic  3.99 us (2%)
    ppermute x20, starting transfers between devices, shift_from(): lax.ppermute(array, axis, [((i + offset) % count, i) for i in range(count)])  88.7 us
    ppermute x20, waiting for transfers between devices, shift_from(): lax.ppermute(array, axis, [((i + offset) % count, i) for i in range(count)])  35.4 us
    pallas_call x7, Pallas kernels, attention(): pl.pallas_call(lambda *refs: attention_kernel(offsets, run_len, count, *r...  33.8 us
  transfers between devices with their start and end apart: 22, of which 5 were waited for; matrix products, arithmetic and copies ran while one was open for 7% of the time, Pallas kernels for 20%

profile of v2, /device:TPU:100, one launch (start us, length us, event | category | flops | bytes accessed | tf_op | source)
XLA Modules:
  0.0 171.6 jit_solution(3295260648020814640)
XLA Ops:
  1.7 24.6 %collective-permute-start = (bf16[1,144,128]{2,1,0:T(8,128)(2,1)S(1)}, bf16[1,144,128]{2,1,0:T(8,128)(2,1)}, u32[]{:S(2)}, u32[]{:S(2)}) collective-permute-start(bf16[1,144,128]{2,1,0:T(8,128)(2,1)S(1)} %pack.1), channel_id=1, source_target_pairs={{12,0},{14,2},{16,4},{18,6},{20,8},{22,10},{24,12},{26,14},{28,16}... | collective-permute-start | bytes 110600 | tf_op jit(solution)/shard_map/ppermute | solution.py:34
  26.3 4.3 %collective-permute-start.1 = (bf16[1,144,128]{2,1,0:T(8,128)(2,1)S(1)}, bf16[1,144,128]{2,1,0:T(8,128)(2,1)S(1)}, u32[]{:S(2)}, u32[]{:S(2)}) collective-permute-start(bf16[1,144,128]{2,1,0:T(8,128)(2,1)S(1)} %pack.1), channel_id=1, source_target_pairs={{26,0},{28,2},{30,4},{32,6},{34,8},{36,10},{38,12},{40,14},{42,16}... | collective-permute-start | bytes 110600 | tf_op jit(solution)/shard_map/ppermute | solution.py:34
  30.6 6.3 %collective-permute-start.3 = (bf16[1,144,128]{2,1,0:T(8,128)(2,1)S(1)}, bf16[1,144,128]{2,1,0:T(8,128)(2,1)}, u32[]{:S(2)}, u32[]{:S(2)}) collective-permute-start(bf16[1,144,128]{2,1,0:T(8,128)(2,1)S(1)} %pack.1), channel_id=1, source_target_pairs={{52,0},{54,2},{56,4},{58,6},{60,8},{62,10},{0,12},{2,14},{4,16},{6... | collective-permute-start | bytes 110600 | tf_op jit(solution)/shard_map/ppermute | solution.py:34
  38.5 2.4 %copy.22 = bf16[96,64,64]{2,1,0:T(8,128)(2,1)S(1)} copy(bf16[96,64,64]{0,2,1:T(8,128)(2,1)S(1)} %bitcast.8) | data formatting | bytes 1572864 | tf_op jit(solution)/shard_map/reshape | solution.py:231
  44.3 4.8 %collective-permute-done.1 = bf16[1,144,128]{2,1,0:T(8,128)(2,1)S(1)} collective-permute-done((bf16[1,144,128]{2,1,0:T(8,128)(2,1)S(1)}, bf16[1,144,128]{2,1,0:T(8,128)(2,1)S(1)}, u32[]{:S(2)}, u32[]{:S(2)}) %collective-permute-start.1) | collective-permute-done | bytes 36896 | tf_op jit(solution)/shard_map/ppermute | solution.py:34
  49.1 2.3 %collective-permute-start.2 = (bf16[1,144,128]{2,1,0:T(8,128)(2,1)S(1)}, bf16[1,144,128]{2,1,0:T(8,128)(2,1)S(1)}, u32[]{:S(2)}, u32[]{:S(2)}) collective-permute-start(bf16[1,144,128]{2,1,0:T(8,128)(2,1)S(1)} %pack.1), channel_id=1, source_target_pairs={{38,0},{40,2},{42,4},{44,6},{46,8},{48,10},{50,12},{52,14},{54,16}... | collective-permute-start | bytes 110600 | tf_op jit(solution)/shard_map/ppermute | solution.py:34
  54.4 17.2 %collective-permute-done.2 = bf16[1,144,128]{2,1,0:T(8,128)(2,1)S(1)} collective-permute-done((bf16[1,144,128]{2,1,0:T(8,128)(2,1)S(1)}, bf16[1,144,128]{2,1,0:T(8,128)(2,1)S(1)}, u32[]{:S(2)}, u32[]{:S(2)}) %collective-permute-start.2) | collective-permute-done | bytes 36896 | tf_op jit(solution)/shard_map/ppermute | solution.py:34
  74.8 6.2 %collective-permute-start.10 = (bf16[5,144,128]{2,1,0:T(8,128)(2,1)S(1)}, bf16[5,144,128]{2,1,0:T(8,128)(2,1)S(1)}, u32[]{:S(2)}, u32[]{:S(2)}) collective-permute-start(bf16[5,144,128]{2,1,0:T(8,128)(2,1)S(1)} %constant_dynamic-update-slice_fusion.refs_1_), channel_id=1, source_target_pairs={{4,0},{6,2},{8,4},{10,6},{12,8},{14,10},{16,12},{18,14},{20,16},{2... | collective-permute-start | bytes 552968 | tf_op jit(solution)/shard_map/ppermute | solution.py:34
  81.8 2.8 %collective-permute-start.14 = (bf16[4,144,128]{2,1,0:T(8,128)(2,1)S(1)}, bf16[4,144,128]{2,1,0:T(8,128)(2,1)S(1)}, u32[]{:S(2)}, u32[]{:S(2)}) collective-permute-start(bf16[4,144,128]{2,1,0:T(8,128)(2,1)S(1)} %pad_maximum_fusion.1), channel_id=1, source_target_pairs={{6,0},{8,2},{10,4},{12,6},{14,8},{16,10},{18,12},{20,14},{22,16},{... | collective-permute-start | bytes 442376 | tf_op jit(solution)/shard_map/ppermute | solution.py:34
  84.6 3.7 %attention.13 = bf16[3,144,128]{2,1,0:T(8,128)(2,1)S(1)} custom-call(s32[257]{0:T(512)S(1)} %pad_add_fusion.1.refs_0_, bf16[3,144,128]{2,1,0:T(8,128)(2,1)S(1)} %collective-permute-done.16.refs_1_, bf16[96,64,512]{2,1,0:T(8,128)(2,1)} %refs_2_.13, bf16[96,64,512]{2,1,0:T(8,128)(2,1)} %collective-permute-done.4.refs_3_, ...), custom_call_target="tpu_custom_call" | custom-call | flops 84934656 | bytes 1474560 | tf_op jit(solution)/shard_map/attention/pallas_call | solution.py:136
  88.3 4.8 %collective-permute-start.17 = (bf16[3,144,128]{2,1,0:T(8,128)(2,1)S(1)}, bf16[3,144,128]{2,1,0:T(8,128)(2,1)S(1)}, u32[]{:S(2)}, u32[]{:S(2)}) collective-permute-start(bf16[3,144,128]{2,1,0:T(8,128)(2,1)S(1)} %attention.13), channel_id=1, source_target_pairs={{6,0},{8,2},{10,4},{12,6},{14,8},{16,10},{18,12},{20,14},{22,16},{... | collective-permute-start | bytes 331784 | tf_op jit(solution)/shard_map/ppermute | solution.py:34
  93.1 5.1 %attention.8 = bf16[5,144,128]{2,1,0:T(8,128)(2,1)S(1)} custom-call(s32[257]{0:T(512)S(1)} %pad_add_fusion.1.refs_0_, bf16[5,144,128]{2,1,0:T(8,128)(2,1)S(1)} %collective-permute-done.6.refs_1_, bf16[96,64,512]{2,1,0:T(8,128)(2,1)} %refs_2_.13, bf16[96,64,512]{2,1,0:T(8,128)(2,1)} %collective-permute-done.4.refs_3_, ...), custom_call_target="tpu_custom_call" | custom-call | flops 141557760 | bytes 2457600 | tf_op jit(solution)/shard_map/attention/pallas_call | solution.py:136
  98.3 5.1 %attention.9 = bf16[5,144,128]{2,1,0:T(8,128)(2,1)S(1)} custom-call(s32[257]{0:T(512)S(1)} %pad_add_fusion.1.refs_0_, bf16[5,144,128]{2,1,0:T(8,128)(2,1)S(1)} %collective-permute-done.8.refs_1_, bf16[96,64,512]{2,1,0:T(8,128)(2,1)} %refs_2_.13, bf16[96,64,512]{2,1,0:T(8,128)(2,1)} %collective-permute-done.4.refs_3_, ...), custom_call_target="tpu_custom_call" | custom-call | flops 141557760 | bytes 2457600 | tf_op jit(solution)/shard_map/attention/pallas_call | solution.py:136
  103.5 2.1 %collective-permute-start.9 = (bf16[5,144,128]{2,1,0:T(8,128)(2,1)S(1)}, bf16[5,144,128]{2,1,0:T(8,128)(2,1)S(1)}, u32[]{:S(2)}, u32[]{:S(2)}) collective-permute-start(bf16[5,144,128]{2,1,0:T(8,128)(2,1)S(1)} %attention.9), channel_id=1, source_target_pairs={{2,0},{4,2},{6,4},{8,6},{10,8},{12,10},{14,12},{16,14},{18,16},{20... | collective-permute-start | bytes 552968 | tf_op jit(solution)/shard_map/ppermute | solution.py:34
  105.6 5.1 %attention.10 = bf16[5,144,128]{2,1,0:T(8,128)(2,1)S(1)} custom-call(s32[257]{0:T(512)S(1)} %pad_add_fusion.1.refs_0_, bf16[5,144,128]{2,1,0:T(8,128)(2,1)S(1)} %collective-permute-done.10.refs_1_, bf16[96,64,512]{2,1,0:T(8,128)(2,1)} %refs_2_.13, bf16[96,64,512]{2,1,0:T(8,128)(2,1)} %collective-permute-done.4.refs_3_, ...), custom_call_target="tpu_custom_call" | custom-call | flops 141557760 | bytes 2457600 | tf_op jit(solution)/shard_map/attention/pallas_call | solution.py:136
  110.9 5.1 %attention.11 = bf16[5,144,128]{2,1,0:T(8,128)(2,1)S(1)} custom-call(s32[257]{0:T(512)S(1)} %pad_add_fusion.1.refs_0_, bf16[5,144,128]{2,1,0:T(8,128)(2,1)S(1)} %collective-permute-done.12.refs_1_, bf16[96,64,512]{2,1,0:T(8,128)(2,1)} %refs_2_.13, bf16[96,64,512]{2,1,0:T(8,128)(2,1)} %collective-permute-done.4.refs_3_, ...), custom_call_target="tpu_custom_call" | custom-call | flops 141557760 | bytes 2457600 | tf_op jit(solution)/shard_map/attention/pallas_call | solution.py:136
  116.0 4.2 %collective-permute-start.13 = (bf16[5,144,128]{2,1,0:T(8,128)(2,1)S(1)}, bf16[5,144,128]{2,1,0:T(8,128)(2,1)S(1)}, u32[]{:S(2)}, u32[]{:S(2)}) collective-permute-start(bf16[5,144,128]{2,1,0:T(8,128)(2,1)S(1)} %attention.11), channel_id=1, source_target_pairs={{4,0},{6,2},{8,4},{10,6},{12,8},{14,10},{16,12},{18,14},{20,16},{2... | collective-permute-start | bytes 552968 | tf_op jit(solution)/shard_map/ppermute | solution.py:34
  120.2 4.4 %attention.12 = bf16[4,144,128]{2,1,0:T(8,128)(2,1)S(1)} custom-call(s32[257]{0:T(512)S(1)} %pad_add_fusion.1.refs_0_, bf16[4,144,128]{2,1,0:T(8,128)(2,1)S(1)} %collective-permute-done.14.refs_1_, bf16[96,64,512]{2,1,0:T(8,128)(2,1)} %refs_2_.13, bf16[96,64,512]{2,1,0:T(8,128)(2,1)} %collective-permute-done.4.refs_3_, ...), custom_call_target="tpu_custom_call" | custom-call | flops 113246208 | bytes 1966080 | tf_op jit(solution)/shard_map/attention/pallas_call | solution.py:136
  126.6 5.1 %attention.7.refs_0_ = bf16[5,144,128]{2,1,0:T(8,128)(2,1)S(1)} custom-call(s32[257]{0:T(512)S(1)} %pad_add_fusion.1.refs_0_, bf16[5,144,128]{2,1,0:T(8,128)(2,1)S(1)} %constant_dynamic-update-slice_fusion.refs_1_, bf16[96,64,512]{2,1,0:T(8,128)(2,1)} %refs_2_.13, bf16[96,64,512]{2,1,0:T(8,128)(2,1)} %collective-permute-done.4.refs_3_, ...), custom_call_target="tpu_custom_call" | custom-call | flops 141557760 | bytes 2457600 | tf_op jit(solution)/shard_map/attention/pallas_call | solution.py:136
  131.7 4.5 %collective-permute-done.15.refs_5_ = bf16[4,144,128]{2,1,0:T(8,128)(2,1)S(1)} collective-permute-done((bf16[4,144,128]{2,1,0:T(8,128)(2,1)S(1)}, bf16[4,144,128]{2,1,0:T(8,128)(2,1)S(1)}, u32[]{:S(2)}, u32[]{:S(2)}) %collective-permute-start.15) | collective-permute-done | bytes 147488 | tf_op jit(solution)/shard_map/ppermute | solution.py:34
  136.8 9.3 %collective-permute-start.19 = (bf16[1,144,128]{2,1,0:T(8,128)(2,1)S(1)}, bf16[1,144,128]{2,1,0:T(8,128)(2,1)S(1)}, u32[]{:S(2)}, u32[]{:S(2)}) collective-permute-start(bf16[1,144,128]{2,1,0:T(8,128)(2,1)S(1)} %get-tuple-element.12), channel_id=1, source_target_pairs={{38,0},{40,2},{42,4},{44,6},{46,8},{48,10},{50,12},{52,14},{54,16}... | collective-permute-start | bytes 110600 | tf_op jit(solution)/shard_map/ppermute | solution.py:34
  146.1 7.3 %collective-permute-start.20 = (bf16[1,144,128]{2,1,0:T(8,128)(2,1)S(1)}, bf16[1,144,128]{2,1,0:T(8,128)(2,1)S(1)}, u32[]{:S(2)}, u32[]{:S(2)}) collective-permute-start(bf16[1,144,128]{2,1,0:T(8,128)(2,1)S(1)} %get-tuple-element.13), channel_id=1, source_target_pairs={{26,0},{28,2},{30,4},{32,6},{34,8},{36,10},{38,12},{40,14},{42,16}... | collective-permute-start | bytes 110600 | tf_op jit(solution)/shard_map/ppermute | solution.py:34
  153.3 8.8 %collective-permute-start.21 = (bf16[1,144,128]{2,1,0:T(8,128)(2,1)S(1)}, bf16[1,144,128]{2,1,0:T(8,128)(2,1)S(1)}, u32[]{:S(2)}, u32[]{:S(2)}) collective-permute-start(bf16[1,144,128]{2,1,0:T(8,128)(2,1)S(1)} %get-tuple-element.14), channel_id=1, source_target_pairs={{12,0},{14,2},{16,4},{18,6},{20,8},{22,10},{24,12},{26,14},{28,16}... | collective-permute-start | bytes 110600 | tf_op jit(solution)/shard_map/ppermute | solution.py:34
  162.2 8.6 %collective-permute-done.20.refs_3_ = bf16[1,144,128]{2,1,0:T(8,128)(2,1)S(1)} collective-permute-done((bf16[1,144,128]{2,1,0:T(8,128)(2,1)S(1)}, bf16[1,144,128]{2,1,0:T(8,128)(2,1)S(1)}, u32[]{:S(2)}, u32[]{:S(2)}) %collective-permute-start.20) | collective-permute-done | bytes 36896 | tf_op jit(solution)/shard_map/ppermute | solution.py:34
  (61 shorter events, 17.2 us)
Async XLA Ops:
  0.0 81.8 %collective-permute-start.4 = (bf16[96,64,512]{2,1,0:T(8,128)(2,1)}, bf16[96,64,512]{2,1,0:T(8,128)(2,1)}, u32[]{:S(2)}, u32[]{:S(2)}) collective-permute-start(bf16[96,64,512]{2,1,0:T(8,128)(2,1)} %refs_2_.13), channel_id=1, source_target_pairs={{0,1},{1,0},{2,3},{3,2},{4,5},{5,4},{6,7},{7,6},{8,9},{9,8},{10,11... | collective-permute-start | bytes 18874376 | tf_op jit(solution)/shard_map/ppermute | solution.py:230
  1.0 0.8 copy-start
  1.7 51.9 %collective-permute-start = (bf16[1,144,128]{2,1,0:T(8,128)(2,1)S(1)}, bf16[1,144,128]{2,1,0:T(8,128)(2,1)}, u32[]{:S(2)}, u32[]{:S(2)}) collective-permute-start(bf16[1,144,128]{2,1,0:T(8,128)(2,1)S(1)} %pack.1), channel_id=1, source_target_pairs={{12,0},{14,2},{16,4},{18,6},{20,8},{22,10},{24,12},{26,14},{28,16}... | collective-permute-start | bytes 110600 | tf_op jit(solution)/shard_map/ppermute | solution.py:34
  26.3 22.8 %collective-permute-start.1 = (bf16[1,144,128]{2,1,0:T(8,128)(2,1)S(1)}, bf16[1,144,128]{2,1,0:T(8,128)(2,1)S(1)}, u32[]{:S(2)}, u32[]{:S(2)}) collective-permute-start(bf16[1,144,128]{2,1,0:T(8,128)(2,1)S(1)} %pack.1), channel_id=1, source_target_pairs={{26,0},{28,2},{30,4},{32,6},{34,8},{36,10},{38,12},{40,14},{42,16}... | collective-permute-start | bytes 110600 | tf_op jit(solution)/shard_map/ppermute | solution.py:34
  30.6 20.8 %collective-permute-start.3 = (bf16[1,144,128]{2,1,0:T(8,128)(2,1)S(1)}, bf16[1,144,128]{2,1,0:T(8,128)(2,1)}, u32[]{:S(2)}, u32[]{:S(2)}) collective-permute-start(bf16[1,144,128]{2,1,0:T(8,128)(2,1)S(1)} %pack.1), channel_id=1, source_target_pairs={{52,0},{54,2},{56,4},{58,6},{60,8},{62,10},{0,12},{2,14},{4,16},{6... | collective-permute-start | bytes 110600 | tf_op jit(solution)/shard_map/ppermute | solution.py:34
  40.9 1.0 copy-start.1
  41.8 39.2 %collective-permute-start.5 = (bf16[96,64,128]{2,1,0:T(8,128)(2,1)S(1)}, bf16[96,64,128]{2,1,0:T(8,128)(2,1)S(1)}, u32[]{:S(2)}, u32[]{:S(2)}) collective-permute-start(bf16[96,64,128]{2,1,0:T(8,128)(2,1)S(1)} %pad_maximum_fusion.refs_4_), channel_id=1, source_target_pairs={{0,1},{1,0},{2,3},{3,2},{4,5},{5,4},{6,7},{7,6},{8,9},{9,8},{10,11... | collective-permute-start | bytes 4718600 | tf_op jit(solution)/shard_map/ppermute | solution.py:233
  49.1 22.6 %collective-permute-start.2 = (bf16[1,144,128]{2,1,0:T(8,128)(2,1)S(1)}, bf16[1,144,128]{2,1,0:T(8,128)(2,1)S(1)}, u32[]{:S(2)}, u32[]{:S(2)}) collective-permute-start(bf16[1,144,128]{2,1,0:T(8,128)(2,1)S(1)} %pack.1), channel_id=1, source_target_pairs={{38,0},{40,2},{42,4},{44,6},{46,8},{48,10},{50,12},{52,14},{54,16}... | collective-permute-start | bytes 110600 | tf_op jit(solution)/shard_map/ppermute | solution.py:34
  52.2 22.6 %collective-permute-start.16 = (bf16[3,144,128]{2,1,0:T(8,128)(2,1)S(1)}, bf16[3,144,128]{2,1,0:T(8,128)(2,1)S(1)}, u32[]{:S(2)}, u32[]{:S(2)}) collective-permute-start(bf16[3,144,128]{2,1,0:T(8,128)(2,1)S(1)} %pad_maximum_fusion.2), channel_id=1, source_target_pairs={{58,0},{60,2},{62,4},{0,6},{2,8},{4,10},{6,12},{8,14},{10,16},{12,... | collective-permute-start | bytes 331784 | tf_op jit(solution)/shard_map/ppermute | solution.py:34
  72.5 15.8 %collective-permute-start.6 = (bf16[5,144,128]{2,1,0:T(8,128)(2,1)S(1)}, bf16[5,144,128]{2,1,0:T(8,128)(2,1)S(1)}, u32[]{:S(2)}, u32[]{:S(2)}) collective-permute-start(bf16[5,144,128]{2,1,0:T(8,128)(2,1)S(1)} %constant_dynamic-update-slice_fusion.refs_1_), channel_id=1, source_target_pairs={{2,0},{4,2},{6,4},{8,6},{10,8},{12,10},{14,12},{16,14},{18,16},{20... | collective-permute-start | bytes 552968 | tf_op jit(solution)/shard_map/ppermute | solution.py:34
  73.4 24.8 %collective-permute-start.8 = (bf16[5,144,128]{2,1,0:T(8,128)(2,1)S(1)}, bf16[5,144,128]{2,1,0:T(8,128)(2,1)S(1)}, u32[]{:S(2)}, u32[]{:S(2)}) collective-permute-start(bf16[5,144,128]{2,1,0:T(8,128)(2,1)S(1)} %constant_dynamic-update-slice_fusion.refs_1_), channel_id=1, source_target_pairs={{62,0},{0,2},{2,4},{4,6},{6,8},{8,10},{10,12},{12,14},{14,16},{16,... | collective-permute-start | bytes 552968 | tf_op jit(solution)/shard_map/ppermute | solution.py:34
  74.8 28.7 %collective-permute-start.10 = (bf16[5,144,128]{2,1,0:T(8,128)(2,1)S(1)}, bf16[5,144,128]{2,1,0:T(8,128)(2,1)S(1)}, u32[]{:S(2)}, u32[]{:S(2)}) collective-permute-start(bf16[5,144,128]{2,1,0:T(8,128)(2,1)S(1)} %constant_dynamic-update-slice_fusion.refs_1_), channel_id=1, source_target_pairs={{4,0},{6,2},{8,4},{10,6},{12,8},{14,10},{16,12},{18,14},{20,16},{2... | collective-permute-start | bytes 552968 | tf_op jit(solution)/shard_map/ppermute | solution.py:34
  81.0 29.7 %collective-permute-start.12 = (bf16[5,144,128]{2,1,0:T(8,128)(2,1)S(1)}, bf16[5,144,128]{2,1,0:T(8,128)(2,1)S(1)}, u32[]{:S(2)}, u32[]{:S(2)}) collective-permute-start(bf16[5,144,128]{2,1,0:T(8,128)(2,1)S(1)} %constant_dynamic-update-slice_fusion.refs_1_), channel_id=1, source_target_pairs={{60,0},{62,2},{0,4},{2,6},{4,8},{6,10},{8,12},{10,14},{12,16},{14,... | collective-permute-start | bytes 552968 | tf_op jit(solution)/shard_map/ppermute | solution.py:34
  81.8 34.2 %collective-permute-start.14 = (bf16[4,144,128]{2,1,0:T(8,128)(2,1)S(1)}, bf16[4,144,128]{2,1,0:T(8,128)(2,1)S(1)}, u32[]{:S(2)}, u32[]{:S(2)}) collective-permute-start(bf16[4,144,128]{2,1,0:T(8,128)(2,1)S(1)} %pad_maximum_fusion.1), channel_id=1, source_target_pairs={{6,0},{8,2},{10,4},{12,6},{14,8},{16,10},{18,12},{20,14},{22,16},{... | collective-permute-start | bytes 442376 | tf_op jit(solution)/shard_map/ppermute | solution.py:34
  88.3 36.4 %collective-permute-start.17 = (bf16[3,144,128]{2,1,0:T(8,128)(2,1)S(1)}, bf16[3,144,128]{2,1,0:T(8,128)(2,1)S(1)}, u32[]{:S(2)}, u32[]{:S(2)}) collective-permute-start(bf16[3,144,128]{2,1,0:T(8,128)(2,1)S(1)} %attention.13), channel_id=1, source_target_pairs={{6,0},{8,2},{10,4},{12,6},{14,8},{16,10},{18,12},{20,14},{22,16},{... | collective-permute-start | bytes 331784 | tf_op jit(solution)/shard_map/ppermute | solution.py:34
  98.2 38.0 %collective-permute-start.7 = (bf16[5,144,128]{2,1,0:T(8,128)(2,1)S(1)}, bf16[5,144,128]{2,1,0:T(8,128)(2,1)S(1)}, u32[]{:S(2)}, u32[]{:S(2)}) collective-permute-start(bf16[5,144,128]{2,1,0:T(8,128)(2,1)S(1)} %attention.8), channel_id=1, source_target_pairs={{62,0},{0,2},{2,4},{4,6},{6,8},{8,10},{10,12},{12,14},{14,16},{16,... | collective-permute-start | bytes 552968 | tf_op jit(solution)/shard_map/ppermute | solution.py:34
  103.5 32.7 %collective-permute-start.9 = (bf16[5,144,128]{2,1,0:T(8,128)(2,1)S(1)}, bf16[5,144,128]{2,1,0:T(8,128)(2,1)S(1)}, u32[]{:S(2)}, u32[]{:S(2)}) collective-permute-start(bf16[5,144,128]{2,1,0:T(8,128)(2,1)S(1)} %attention.9), channel_id=1, source_target_pairs={{2,0},{4,2},{6,4},{8,6},{10,8},{12,10},{14,12},{16,14},{18,16},{20... | collective-permute-start | bytes 552968 | tf_op jit(solution)/shard_map/ppermute | solution.py:34
  110.7 25.5 %collective-permute-start.11 = (bf16[5,144,128]{2,1,0:T(8,128)(2,1)S(1)}, bf16[5,144,128]{2,1,0:T(8,128)(2,1)S(1)}, u32[]{:S(2)}, u32[]{:S(2)}) collective-permute-start(bf16[5,144,128]{2,1,0:T(8,128)(2,1)S(1)} %attention.10), channel_id=1, source_target_pairs={{60,0},{62,2},{0,4},{2,6},{4,8},{6,10},{8,12},{10,14},{12,16},{14,... | collective-permute-start | bytes 552968 | tf_op jit(solution)/shard_map/ppermute | solution.py:34
  116.0 20.2 %collective-permute-start.13 = (bf16[5,144,128]{2,1,0:T(8,128)(2,1)S(1)}, bf16[5,144,128]{2,1,0:T(8,128)(2,1)S(1)}, u32[]{:S(2)}, u32[]{:S(2)}) collective-permute-start(bf16[5,144,128]{2,1,0:T(8,128)(2,1)S(1)} %attention.11), channel_id=1, source_target_pairs={{4,0},{6,2},{8,4},{10,6},{12,8},{14,10},{16,12},{18,14},{20,16},{2... | collective-permute-start | bytes 552968 | tf_op jit(solution)/shard_map/ppermute | solution.py:34
  124.7 11.5 %collective-permute-start.15 = (bf16[4,144,128]{2,1,0:T(8,128)(2,1)S(1)}, bf16[4,144,128]{2,1,0:T(8,128)(2,1)S(1)}, u32[]{:S(2)}, u32[]{:S(2)}) collective-permute-start(bf16[4,144,128]{2,1,0:T(8,128)(2,1)S(1)} %attention.12), channel_id=1, source_target_pairs={{58,0},{60,2},{62,4},{0,6},{2,8},{4,10},{6,12},{8,14},{10,16},{12,... | collective-permute-start | bytes 442376 | tf_op jit(solution)/shard_map/ppermute | solution.py:34
  136.6 25.5 %collective-permute-start.18 = (bf16[1,144,128]{2,1,0:T(8,128)(2,1)S(1)}, bf16[1,144,128]{2,1,0:T(8,128)(2,1)S(1)}, u32[]{:S(2)}, u32[]{:S(2)}) collective-permute-start(bf16[1,144,128]{2,1,0:T(8,128)(2,1)S(1)} %get-tuple-element.11), channel_id=1, source_target_pairs={{52,0},{54,2},{56,4},{58,6},{60,8},{62,10},{0,12},{2,14},{4,16},{6... | collective-permute-start | bytes 110600 | tf_op jit(solution)/shard_map/ppermute | solution.py:34
  136.8 25.4 %collective-permute-start.19 = (bf16[1,144,128]{2,1,0:T(8,128)(2,1)S(1)}, bf16[1,144,128]{2,1,0:T(8,128)(2,1)S(1)}, u32[]{:S(2)}, u32[]{:S(2)}) collective-permute-start(bf16[1,144,128]{2,1,0:T(8,128)(2,1)S(1)} %get-tuple-element.12), channel_id=1, source_target_pairs={{38,0},{40,2},{42,4},{44,6},{46,8},{48,10},{50,12},{52,14},{54,16}... | collective-permute-start | bytes 110600 | tf_op jit(solution)/shard_map/ppermute | solution.py:34
  146.1 24.6 %collective-permute-start.20 = (bf16[1,144,128]{2,1,0:T(8,128)(2,1)S(1)}, bf16[1,144,128]{2,1,0:T(8,128)(2,1)S(1)}, u32[]{:S(2)}, u32[]{:S(2)}) collective-permute-start(bf16[1,144,128]{2,1,0:T(8,128)(2,1)S(1)} %get-tuple-element.13), channel_id=1, source_target_pairs={{26,0},{28,2},{30,4},{32,6},{34,8},{36,10},{38,12},{40,14},{42,16}... | collective-permute-start | bytes 110600 | tf_op jit(solution)/shard_map/ppermute | solution.py:34
  153.3 17.4 %collective-permute-start.21 = (bf16[1,144,128]{2,1,0:T(8,128)(2,1)S(1)}, bf16[1,144,128]{2,1,0:T(8,128)(2,1)S(1)}, u32[]{:S(2)}, u32[]{:S(2)}) collective-permute-start(bf16[1,144,128]{2,1,0:T(8,128)(2,1)S(1)} %get-tuple-element.14), channel_id=1, source_target_pairs={{12,0},{14,2},{16,4},{18,6},{20,8},{22,10},{24,12},{26,14},{28,16}... | collective-permute-start | bytes 110600 | tf_op jit(solution)/shard_map/ppermute | solution.py:34
